TPU v7x, 32 devices: a whole 2x2x4 slice. The times are simulated.
32 devices in a mesh: gx: 4 (over x, core), yz: 8 (over z, y).
Axes of the slice: x: 2, y: 2, z: 4, core: 2. Of those that a mesh axis runs over, the one named last changes fastest.
Arguments:
- pressure: bfloat16 [8192, 4096], P(('gx', 'yz')), may hold values from -6 to 6
- face_block: int32 [131072], P(('gx', 'yz')), may hold values from 0 to 255
- stencil_local: int32 [32, 131072], P(None, ('gx', 'yz')), may hold values from 0 to 4095
- stencil_weight: float32 [32, 131072], P(None, ('gx', 'yz')), may hold values from 0 to 0.25
- area_normal: float32 [12, 131072], P(None, ('gx', 'yz')), may hold values from -6 to 6
- face_part: int32 [131072, 1], P(('gx', 'yz')), may hold values from 0 to 31; in each aligned block of 4096 rows (0 to 4095, 4096 to 8191, ...) at most 256 rows name the same one
- face_nodes: int32 [8, 131072], P(None, ('gx', 'yz')), may hold values from 0 to 1023
- stiffness: float32 [60, 60, 8192], P(None, None, ('gx', 'yz')), may hold values from -0.075 to 6, as said below
- connect: int32 [20, 8192], P(None, ('gx', 'yz')), may hold values from 0 to 1279
- halo_nodes: int32 [2, 4096], P(None, ('gx', 'yz')), may hold values from 0 to 1023
- node_mass: float32 [32768], P(('gx', 'yz')), may hold values from 24 to 160
- displacement: float32 [3, 32768], P(None, ('gx', 'yz')), may hold values from -6 to 6
- velocity: float32 [3, 32768], P(None, ('gx', 'yz')), may hold values from -3 to 3
Outputs:
- node_disp: float32 [3, 32768], P(None, ('gx', 'yz'))
- face_disp: float32 [12, 131072], P(None, ('gx', 'yz'))
Inputs may be any that keep to these rules, and one draw needn't show every extreme that they name: `face_part`: the faces of one device name no partition more than 256 times; in every draw some device names some partition exactly 256 times. `connect`: local node l of a partition: l < 1024 is owned, 1024 + g is entry g of the previous partition's row 1, 1152 + g entry g of the next partition's row 0 (along gx+yz). `halo_nodes`: each partition's 128 entries of row 0 are owned nodes held as ghosts by the previous partition, row 1 by the next; entries may repeat. `stiffness`: each element's matrix is symmetric positive definite.
All inputs are finite; a program needn't handle non-finite values.
Results may differ from a plain program's by a relative error of at most 0.0003.
Values sent between devices are 32-bit elements; how exact they have to be, the bound alone decides.
A program may use at most 256 MiB of HBM per device.

v0:
```python
import functools
import math

import jax
import jax.numpy as jnp
import numpy as np
from jax import lax
from jax.experimental import pallas as pl
from jax.experimental.pallas import tpu as pltpu
from jax.sharding import PartitionSpec as P

SUBSTEPS = 4


def shape_table():
    corner_u = [-1, 1, 1, -1, 0, 1, 0, -1]
    corner_v = [-1, -1, 1, 1, -1, 0, 1, 0]
    gauss_point = 1.0 / math.sqrt(3.0)
    points = [
        (-gauss_point, -gauss_point),
        (gauss_point, -gauss_point),
        (gauss_point, gauss_point),
        (-gauss_point, gauss_point),
    ]
    shape_values = np.zeros((4, 8), np.float32)
    for position, (coord_u, coord_v) in enumerate(points):
        for corner in range(8):
            node_u = corner_u[corner]
            node_v = corner_v[corner]
            if corner < 4:
                entry_value = (
                    0.25
                    * (1 + coord_u * node_u)
                    * (1 + coord_v * node_v)
                    * (coord_u * node_u + coord_v * node_v - 1)
                )
            elif node_u == 0:
                entry_value = 0.5 * (1 - coord_u * coord_u) * (1 + coord_v * node_v)
            else:
                entry_value = 0.5 * (1 + coord_u * node_u) * (1 - coord_v * coord_v)
            shape_values[position, corner] = entry_value
    return shape_values


def hot_pair(indices, extent):
    lanes_width = 32
    upper_count = -(-extent // lanes_width)
    upper_hot = (
        indices[None, :] // lanes_width == lax.broadcasted_iota(jnp.int32, (upper_count, 1), 0)
    ).astype(jnp.float32)
    lower_hot = (
        indices[None, :] % lanes_width == lax.broadcasted_iota(jnp.int32, (lanes_width, 1), 0)
    ).astype(jnp.float32)
    return (upper_hot, lower_hot)


def spread_cols(values, hots):
    upper_hot, lower_hot = hots
    lanes_width = lower_hot.shape[0]
    upper_count = upper_hot.shape[0]
    comps = values.shape[0]
    masked = (values[:, None, :] * lower_hot[None]).reshape(comps * lanes_width, -1)
    summed = lax.dot_general(
        masked,
        upper_hot,
        (((1,), (1,)), ((), ())),
        precision=lax.Precision.HIGHEST,
        preferred_element_type=jnp.float32,
    )
    return (
        summed.reshape(comps, lanes_width, upper_count)
        .transpose(0, 2, 1)
        .reshape(comps, upper_count * lanes_width)
    )


def arrival_order(target, devices):
    row_count = target.shape[0]
    group_rows = min(512, row_count)
    groups = row_count // group_rows
    onehot = (target[:, None] == jnp.arange(devices, dtype=jnp.int32)[None, :]).astype(jnp.bfloat16)
    onehot = onehot.reshape(groups, group_rows, devices)
    lower_ones = (
        lax.broadcasted_iota(jnp.int32, (group_rows, group_rows), 0)
        > lax.broadcasted_iota(jnp.int32, (group_rows, group_rows), 1)
    ).astype(jnp.bfloat16)
    before = jnp.einsum("ij,gjd->gid", lower_ones, onehot, preferred_element_type=jnp.float32)
    onehot_float = onehot.astype(jnp.float32)
    totals = jnp.sum(onehot_float, axis=1)
    offsets = jnp.cumsum(totals, axis=0) - totals
    placed = jnp.sum((before + offsets[:, None, :]) * onehot_float, axis=2)
    return placed.reshape(row_count).astype(jnp.int32)


LANES = 128
SUBLANES = 8


def gather_entries(hot, table, entries, rows_ref, low_ref, high_ref, value_ref):
    tile = hot.shape[0]
    entry_count = entries.shape[0]
    chunks = table.shape[1] // LANES
    rows_ref[...] = jnp.dot(hot, table, preferred_element_type=jnp.float32)
    padded = jnp.concatenate(
        [entries, jnp.zeros((LANES - entry_count, tile), jnp.int32)], axis=0
    ).T
    low_ref[...] = lax.rem(padded, LANES)
    high_ref[...] = lax.div(padded, LANES)

    def group(step, carry):
        rows = pl.ds(pl.multiple_of(step * SUBLANES, SUBLANES), SUBLANES)
        low = low_ref[rows, :]
        high = high_ref[rows, :]
        taken = jnp.zeros((SUBLANES, LANES), jnp.float32)
        for chunk in range(chunks):
            part = rows_ref[rows, chunk * LANES : (chunk + 1) * LANES]
            part = jnp.take_along_axis(part, low, axis=1, mode="promise_in_bounds")
            taken = jnp.where(high == chunk, part, taken)
        value_ref[rows, :] = taken
        return carry

    lax.fori_loop(0, tile // SUBLANES, group, 0, unroll=8)
    return value_ref[...].T[:entry_count]


def hot_rows(labels, count):
    tile = labels.shape[1]
    hot = lax.broadcasted_iota(jnp.int32, (count, tile), 0) == labels
    return hot.astype(jnp.float32).T.astype(jnp.bfloat16)


def traction_kernel(block_ref, local_ref, weight_ref, normal_ref, pressure_ref, out_ref, *scratch):
    hot = hot_rows(block_ref[...], pressure_ref.shape[0])
    cells = gather_entries(hot, pressure_ref[...], local_ref[...], *scratch)
    weighted = weight_ref[...] * cells
    tile = weighted.shape[1]
    points = out_ref.shape[0] // 3
    face_pressure = jnp.sum(weighted.reshape(points, -1, tile), axis=1)
    face_pressure = jnp.concatenate([face_pressure] * 3, axis=0)
    out_ref[...] = -(normal_ref[...] * face_pressure)


def return_kernel(part_ref, nodes_ref, shape_ref, table_ref, out_ref, *scratch):
    count, width = table_ref.shape
    table = table_ref[...]
    head = table.astype(jnp.bfloat16)
    tail = (table - head.astype(jnp.float32)).astype(jnp.bfloat16)
    hot = hot_rows(part_ref[...], count)
    owned = width // 3
    nodes = nodes_ref[...]
    entries = jnp.concatenate([nodes, nodes + owned, nodes + 2 * owned], axis=0)
    at_nodes = gather_entries(
        jnp.concatenate([hot, hot], axis=1), jnp.concatenate([head, tail], axis=0), entries, *scratch
    )
    out_ref[...] = jnp.dot(
        shape_ref[...],
        at_nodes,
        precision=lax.Precision.HIGHEST,
        preferred_element_type=jnp.float32,
    )


def face_tile(face_count):
    return math.gcd(face_count, 256)


def tile_scratch(tile, width):
    return [
        pltpu.VMEM((tile, width), jnp.float32),
        pltpu.VMEM((tile, LANES), jnp.int32),
        pltpu.VMEM((tile, LANES), jnp.int32),
        pltpu.VMEM((tile, LANES), jnp.float32),
    ]


def column_spec(rows, tile):
    return pl.BlockSpec((rows, tile), lambda step: (0, step))


def whole_spec(array):
    return pl.BlockSpec(array.shape, lambda step: (0, 0))


def stencil_traction(pressure, face_block, stencil_local, stencil_weight, area_normal):
    face_count = face_block.shape[0]
    tile = face_tile(face_count)
    flops = 2 * face_count * pressure.size
    return pl.pallas_call(
        traction_kernel,
        grid=(face_count // tile,),
        in_specs=[
            column_spec(1, tile),
            column_spec(stencil_local.shape[0], tile),
            column_spec(stencil_weight.shape[0], tile),
            column_spec(area_normal.shape[0], tile),
            whole_spec(pressure),
        ],
        out_specs=column_spec(area_normal.shape[0], tile),
        out_shape=jax.ShapeDtypeStruct(area_normal.shape, jnp.float32),
        scratch_shapes=tile_scratch(tile, pressure.shape[1]),
        cost_estimate=pl.CostEstimate(flops=flops, bytes_accessed=4 * pressure.size, transcendentals=0),
    )(face_block.reshape(1, -1), stencil_local, stencil_weight, area_normal, pressure)


def wall_points(table, face_part, face_nodes):
    face_count = face_nodes.shape[1]
    tile = face_tile(face_count)
    shapes = shape_table()
    blocks = np.zeros((3 * shapes.shape[0], 3 * shapes.shape[1]), np.float32)
    for comp in range(3):
        blocks[comp * 4 : comp * 4 + 4, comp * 8 : comp * 8 + 8] = shapes
    blocks = jnp.asarray(blocks)
    flops = 4 * face_count * table.size
    return pl.pallas_call(
        return_kernel,
        grid=(face_count // tile,),
        in_specs=[
            column_spec(1, tile),
            column_spec(face_nodes.shape[0], tile),
            whole_spec(blocks),
            whole_spec(table),
        ],
        out_specs=column_spec(blocks.shape[0], tile),
        out_shape=jax.ShapeDtypeStruct((blocks.shape[0], face_count), jnp.float32),
        scratch_shapes=tile_scratch(tile, table.shape[1]),
        cost_estimate=pl.CostEstimate(flops=flops, bytes_accessed=4 * table.size, transcendentals=0),
    )(face_part.reshape(1, -1), face_nodes, blocks, table)


def split_rows(rows):
    head = rows.astype(jnp.bfloat16)
    tail = (rows - head.astype(jnp.float32)).astype(jnp.bfloat16)
    return jnp.concatenate([head, tail], axis=0)


def spread_dot(rows, hot):
    both = lax.dot_general(
        split_rows(rows), hot, (((1,), (1,)), ((), ())), preferred_element_type=jnp.float32
    )
    return both[: rows.shape[0]] + both[rows.shape[0] :]


def solid_kernel(
    axis_sizes,
    stiff_ref,
    low_ref,
    high_ref,
    upper_ref,
    lower_ref,
    halo_low_ref,
    halo_high_ref,
    halo_upper_ref,
    halo_lower_ref,
    external_ref,
    mass_ref,
    disp_ref,
    vel_ref,
    table_ref,
    final_ref,
    send_ref,
    recv_ref,
    local_ref,
    force_ref,
    send_sem,
    recv_sem,
    wide_send_sem,
    wide_recv_sem,
):
    gx_size, yz_size = axis_sizes
    devices = gx_size * yz_size
    here = lax.axis_index("gx") * yz_size + lax.axis_index("yz")
    has_prev = here > 0
    has_next = here < devices - 1
    owned_rows = mass_ref.shape[0]
    freedom = stiff_ref.shape[0]
    nodes = freedom // 3
    padded_rows = upper_ref.shape[1]
    table_rows = owned_rows + 2
    halves = stiff_ref.shape[2] // LANES

    def place(device):
        return {"gx": lax.div(device, yz_size), "yz": lax.rem(device, yz_size)}

    def to_side(turn, side):
        return pltpu.make_async_remote_copy(
            src_ref=send_ref.at[turn, side],
            dst_ref=recv_ref.at[turn, 1 - side],
            send_sem=send_sem.at[turn, side],
            recv_sem=recv_sem.at[turn, 1 - side],
            device_id=place(here + 2 * side - 1),
            device_id_type=pl.DeviceIdType.MESH,
        )

    def swap(turn):
        @pl.when(has_prev)
        def _():
            to_side(turn, 0).start()

        @pl.when(has_next)
        def _():
            to_side(turn, 1).start()

        @pl.when(has_prev)
        def _():
            to_side(turn, 0).wait_send()
            to_side(turn, 1).wait_recv()

        @pl.when(has_next)
        def _():
            to_side(turn, 1).wait_send()
            to_side(turn, 0).wait_recv()

    blank = jnp.zeros((recv_ref.shape[0],) + recv_ref.shape[2:], jnp.float32)
    send_ref[:, 0] = blank
    send_ref[:, 1] = blank

    @pl.when(jnp.logical_not(has_prev))
    def _():
        recv_ref[:, 0] = blank

    @pl.when(jnp.logical_not(has_next))
    def _():
        recv_ref[:, 1] = blank

    def pick(row, low):
        row = jnp.broadcast_to(row, low.shape)
        return jnp.take_along_axis(row, low, axis=1, mode="promise_in_bounds")

    def substep(step, carry):
        disp, vel = carry
        turn = 2 * step
        halo_low = halo_low_ref[...]
        halo_high = halo_high_ref[...]
        for comp in range(3):
            taken = jnp.zeros(halo_low.shape, jnp.float32)
            for row in range(owned_rows):
                part = pick(disp[comp][row : row + 1], halo_low)
                taken = jnp.where(halo_high == row, part, taken)
            for side in range(2):
                send_ref[turn, side, comp : comp + 1, :] = taken[side : side + 1]
        swap(turn)
        ghosts = [recv_ref[turn, side] for side in range(2)]
        for start in range(0, low_ref.shape[0], SUBLANES):
            last = min(start + SUBLANES, freedom) - 1
            for half in range(halves):
                lanes = slice(half * LANES, (half + 1) * LANES)
                low = low_ref[start : start + SUBLANES, lanes]
                high = high_ref[start : start + SUBLANES, lanes]
                taken = jnp.zeros(low.shape, jnp.float32)
                for comp in range(start // nodes, last // nodes + 1):
                    for row in range(table_rows):
                        if row < owned_rows:
                            source = disp[comp][row : row + 1]
                        else:
                            source = ghosts[row - owned_rows][comp : comp + 1]
                        part = pick(source, low)
                        taken = jnp.where(high == comp * table_rows + row, part, taken)
                local_ref[start : start + SUBLANES, lanes] = taken
        local = local_ref[:freedom, :]
        for row in range(freedom):
            force_ref[row : row + 1, :] = jnp.sum(stiff_ref[row] * local, axis=0, keepdims=True)
        spread = jnp.zeros((3 * padded_rows, LANES), jnp.float32)
        for node in range(nodes):
            rows = [
                force_ref[comp * nodes + node : comp * nodes + node + 1, :] * upper_ref[node]
                for comp in range(3)
            ]
            spread = spread + spread_dot(jnp.concatenate(rows, axis=0), lower_ref[node])
        for comp in range(3):
            for side in range(2):
                row = comp * padded_rows + owned_rows + side
                send_ref[turn + 1, side, comp : comp + 1, :] = spread[row : row + 1]
        swap(turn + 1)
        internal = [
            spread[comp * padded_rows : comp * padded_rows + owned_rows] for comp in range(3)
        ]
        for side in range(2):
            arrived = recv_ref[turn + 1, side]
            rows = [arrived[comp : comp + 1] * halo_upper_ref[side] for comp in range(3)]
            added = spread_dot(jnp.concatenate(rows, axis=0), halo_lower_ref[side])
            internal = [
                internal[comp] + added[comp * owned_rows : (comp + 1) * owned_rows]
                for comp in range(3)
            ]
        vel = tuple(
            vel[comp] + (external_ref[comp] - internal[comp]) / mass_ref[...] for comp in range(3)
        )
        disp = tuple(disp[comp] + vel[comp] for comp in range(3))
        return disp, vel

    start = (
        tuple(disp_ref[comp] for comp in range(3)),
        tuple(vel_ref[comp] for comp in range(3)),
    )
    disp, _ = lax.fori_loop(0, SUBSTEPS, substep, start)
    for comp in range(3):
        final_ref[comp * owned_rows : (comp + 1) * owned_rows, :] = disp[comp]
    table_ref[here] = jnp.concatenate(list(disp), axis=0)

    def to_device(step):
        return pltpu.make_async_remote_copy(
            src_ref=final_ref,
            dst_ref=table_ref.at[here],
            send_sem=wide_send_sem.at[step],
            recv_sem=wide_recv_sem.at[step],
            device_id=place(lax.rem(here + step, devices)),
            device_id_type=pl.DeviceIdType.MESH,
        )

    def send_one(step, carry):
        to_device(step).start()
        return carry

    def wait_one(step, carry):
        to_device(step).wait()
        return carry

    lax.fori_loop(1, devices, send_one, 0)
    lax.fori_loop(1, devices, wait_one, 0)


def one_hot(labels, count, kind):
    shape = labels.shape[:-1] + (count, labels.shape[-1])
    return (lax.broadcasted_iota(jnp.int32, shape, len(shape) - 2) == labels[..., None, :]).astype(kind)


def solid_steps(stiffness, connect, halo_nodes, external, node_mass, displacement, velocity):
    gx_size = lax.axis_size("gx")
    yz_size = lax.axis_size("yz")
    devices = gx_size * yz_size
    owned_rows = displacement.shape[1] // LANES
    padded_rows = -(-(owned_rows + 2) // SUBLANES) * SUBLANES
    freedom, _, elements = stiffness.shape
    span = (owned_rows + 2) * LANES
    entries = jnp.concatenate([connect, connect + span, connect + 2 * span], axis=0)
    entries = jnp.pad(entries, ((0, -freedom % SUBLANES), (0, 0)))
    halo = jnp.pad(halo_nodes, ((0, -halo_nodes.shape[0] % SUBLANES), (0, 0)))
    ghosts = halo_nodes.shape[1]
    turns = 2 * SUBSTEPS
    operands = (
        stiffness,
        entries % LANES,
        entries // LANES,
        one_hot(connect // LANES, padded_rows, jnp.float32),
        one_hot(connect % LANES, LANES, jnp.bfloat16),
        halo % LANES,
        halo // LANES,
        one_hot(halo_nodes // LANES, owned_rows, jnp.float32),
        one_hot(halo_nodes % LANES, LANES, jnp.bfloat16),
        external.reshape(3, owned_rows, LANES),
        node_mass.reshape(owned_rows, LANES),
        displacement.reshape(3, owned_rows, LANES),
        velocity.reshape(3, owned_rows, LANES),
    )
    vmem = pl.BlockSpec(memory_space=pltpu.VMEM)
    return pl.pallas_call(
        functools.partial(solid_kernel, (gx_size, yz_size)),
        in_specs=[vmem] * len(operands),
        out_specs=[vmem] * 2,
        out_shape=[
            jax.ShapeDtypeStruct((devices, 3 * owned_rows, LANES), jnp.float32),
            jax.ShapeDtypeStruct((3 * owned_rows, LANES), jnp.float32),
        ],
        scratch_shapes=[
            pltpu.VMEM((turns, 2, SUBLANES, ghosts), jnp.float32),
            pltpu.VMEM((turns, 2, SUBLANES, ghosts), jnp.float32),
            pltpu.VMEM((entries.shape[0], elements), jnp.float32),
            pltpu.VMEM((entries.shape[0], elements), jnp.float32),
            pltpu.SemaphoreType.DMA((turns, 2)),
            pltpu.SemaphoreType.DMA((turns, 2)),
            pltpu.SemaphoreType.DMA((devices,)),
            pltpu.SemaphoreType.DMA((devices,)),
        ],
        compiler_params=pltpu.CompilerParams(has_side_effects=True),
        cost_estimate=pl.CostEstimate(
            flops=2 * SUBSTEPS * stiffness.size, bytes_accessed=4 * stiffness.size, transcendentals=0
        ),
    )(*operands)


def shards(
    pressure,
    face_block,
    stencil_local,
    stencil_weight,
    area_normal,
    face_part,
    face_nodes,
    stiffness,
    connect,
    halo_nodes,
    node_mass,
    displacement,
    velocity,
):
    highest = lax.Precision.HIGHEST
    gx_size = lax.axis_size("gx")
    yz_size = lax.axis_size("yz")
    devices = gx_size * yz_size
    shapes = jnp.asarray(shape_table(), dtype=jnp.float32)
    face_count = face_block.shape[0]
    capacity = max(2, 2 * face_count // devices)
    slot_total = devices * capacity
    traction = stencil_traction(pressure, face_block, stencil_local, stencil_weight, area_normal)
    target = face_part[:, 0]
    slots = target * capacity + arrival_order(target, devices)
    slot_hots = hot_pair(slots, slot_total)
    packed = spread_cols(
        jnp.concatenate([traction, face_nodes.astype(jnp.float32)], axis=0), slot_hots
    )
    load_buffer = packed[:12].reshape(12, devices, capacity)
    node_buffer = packed[12:].reshape(8, devices, capacity)
    arrived_load, arrived_nodes = (
        lax.all_to_all(load_buffer, ("gx", "yz"), split_axis=1, concat_axis=1, tiled=True),
        lax.all_to_all(node_buffer, ("gx", "yz"), split_axis=1, concat_axis=1, tiled=True),
    )
    received = arrived_load.reshape(3, 4, slot_total)
    node_ids = arrived_nodes.reshape(8 * slot_total).astype(jnp.int32)
    owned_count = displacement.shape[1]
    node_hots = hot_pair(node_ids, owned_count)
    load = jnp.einsum("qa,cqs->cas", shapes, received, precision=highest)
    external = spread_cols(load.reshape(3, -1), node_hots)
    table, final = solid_steps(
        stiffness, connect, halo_nodes, external, node_mass, displacement, velocity
    )
    node_disp = final.reshape(displacement.shape)
    face_disp = wall_points(table.reshape(devices, 3 * owned_count), face_part, face_nodes)
    return (node_disp, face_disp)


def solution(mesh):
    in_specs = (
        P(("gx", "yz"), None),
        P(("gx", "yz")),
        P(None, ("gx", "yz")),
        P(None, ("gx", "yz")),
        P(None, ("gx", "yz")),
        P(("gx", "yz"), None),
        P(None, ("gx", "yz")),
        P(None, None, ("gx", "yz")),
        P(None, ("gx", "yz")),
        P(None, ("gx", "yz")),
        P(("gx", "yz")),
        P(None, ("gx", "yz")),
        P(None, ("gx", "yz")),
    )
    out_specs = (P(None, ("gx", "yz")), P(None, ("gx", "yz")))
    return jax.shard_map(shards, mesh=mesh, in_specs=in_specs, out_specs=out_specs, check_vma=False)
```

profile of v0, /device:TPU:1, one launch (start us, length us, event | category | flops | bytes accessed | tf_op | source)
XLA Modules:
  0.0 201.4 jit_solution(2969940228695459516)
XLA Ops:
  1.1 1.4 fusion.50
  3.2 0.9 convert_element_type.69
  4.1 39.5 %shard_map.158 = f32[12,4096]{1,0:T(8,128)} custom-call(s32[1,4096]{1,0:T(1,128)} %bitcast.61, s32[32,4096]{1,0:T(8,128)} %local_ref.1, f32[32,4096]{1,0:T(8,128)} %weight_ref.1, f32[12,4096]{1,0:T(8,128)} %normal_ref.1, bf16[256,4096]{1,0:T(8,128)(2,1)} %pressure_ref.1), custom_call_target="tpu_custom_call" | custom-call | flops 8589934592 | bytes 4194304 | tf_op jit(solution)/shard_map/pallas_call | solution.py:188
  43.6 1.0 pad_maximum_fusion
  44.6 5.7 %fusion.16 = f32[20,256,32]{1,2,0:T(8,128)S(1)} fusion(s32[4096]{0:T(1024)S(1)} %get-tuple-element.11, f32[32,4096]{1,0:T(8,128)S(1)} %fusion.32, f32[20,4096]{1,0:T(8,128)S(1)} %pad_maximum_fusion), kind=kOutput, calls=%fused_computation.19 | convolution fusion | flops 8056733696 | bytes 1523712 | tf_op jit(solution)/shard_map/dot_general | solution.py:63
  51.1 0.9 copy.31
  51.9 7.1 %all-to-all-start.1 = ((f32[8,32,256]{2,0,1:T(8,128)}), f32[8,32,256]{2,0,1:T(8,128)S(1)}, u32[]{:S(2)}, u32[]{:S(2)}) async-start(f32[8,32,256]{2,0,1:T(8,128)} %copy.31), calls=%async_computation.1 | async-start | bytes 524288 | tf_op jit(solution)/shard_map/all_to_all | solution.py:515
  59.1 0.7 add_select_fusion.2
  59.8 0.6 fusion.37.halo_lower_ref
  61.1 0.6 copy_bitcast_fusion.1
  63.2 1.0 copy.28
  64.3 0.8 fusion.33.upper_ref
  65.1 1.6 fusion.14.lower_ref
  66.7 2.5 %all-to-all-done.1 = f32[8,32,256]{2,0,1:T(8,128)S(1)} async-done(((f32[8,32,256]{2,0,1:T(8,128)}), f32[8,32,256]{2,0,1:T(8,128)S(1)}, u32[]{:S(2)}, u32[]{:S(2)}) %all-to-all-start.1) | async-done | bytes 262176 | tf_op jit(solution)/shard_map/all_to_all | solution.py:515
  69.2 3.5 %all-to-all-start = ((f32[12,32,256]{2,0,1:T(8,128)}), f32[12,32,256]{2,0,1:T(8,128)S(1)}, u32[]{:S(2)}, u32[]{:S(2)}) async-start(f32[12,32,256]{2,0,1:T(8,128)} %copy.28), calls=%async_computation | async-start | bytes 1048576 | tf_op jit(solution)/shard_map/all_to_all | solution.py:514
  73.2 3.8 %fusion.6 = f32[32,65536]{1,0:T(8,128)} fusion(s32[65536]{0:T(1024)S(1)} %get-tuple-element.6), kind=kLoop, calls=%fused_computation.9 | loop fusion | flops 4194304 | bytes 8650752 | tf_op jit(solution)/shard_map/convert_element_type | solution.py:53
  77.0 11.3 %all-to-all-done = f32[12,32,256]{2,0,1:T(8,128)S(1)} async-done(((f32[12,32,256]{2,0,1:T(8,128)}), f32[12,32,256]{2,0,1:T(8,128)S(1)}, u32[]{:S(2)}, u32[]{:S(2)}) %all-to-all-start) | async-done | bytes 393248 | tf_op jit(solution)/shard_map/all_to_all | solution.py:514
  88.7 0.8 convolution_bitcast_fusion
  90.1 16.7 %fusion.24 = f32[3,32,32]{1,2,0:T(8,128)S(1)} fusion(s32[65536]{0:T(1024)S(1)} %get-tuple-element.7, f32[32,65536]{1,0:T(8,128)} %fusion.6, f32[3,65536]{1,0:T(4,128)S(1)} %bitcast.50), kind=kOutput, calls=%fused_computation.24 | convolution fusion | flops 2424307712 | bytes 9449472 | tf_op jit(solution)/shard_map/dot_general | solution.py:63
  106.9 0.7 reshape_reshape.3.external_ref
  107.6 53.4 %shard_map.159 = (f32[32,24,128]{2,1,0:T(8,128)}, f32[24,128]{1,0:T(8,128)}) custom-call(f32[60,60,256]{2,1,0:T(8,128)} %stiff_ref.1, s32[64,256]{1,0:T(8,128)} %get-tuple-element.9.low_ref, s32[64,256]{1,0:T(8,128)} %get-tuple-element.8.high_ref, f32[20,16,256]{2,1,0:T(8,128)} %fusion.33.upper_ref, bf16[20,128,256]{2,1,0:T(8,128)(2,1)} %fusion.14.lower_ref, ...), custom_call_target="tpu_custom_call" | custom-call | flops 7372800 | bytes 3686400 | tf_op jit(solution)/shard_map/pallas_call | solution.py:456
  161.0 1.8 copy.43
  162.9 1.3 reshape.259
  164.2 37.2 %shard_map.160 = f32[12,4096]{1,0:T(8,128)} custom-call(s32[1,4096]{1,0:T(1,128)} %bitcast.59, s32[8,4096]{1,0:T(8,128)} %nodes_ref.1, f32[12,24]{1,0:T(8,128)} %constant.138.clone.shape_ref, f32[32,3072]{1,0:T(8,128)} %bitcast.54), custom_call_target="tpu_custom_call" | custom-call | flops 1610612736 | bytes 393216 | tf_op jit(solution)/shard_map/pallas_call | solution.py:214
  (39 shorter events, 5.5 us)
Async XLA Ops:
  43.6 15.4 %copy-start = (s32[20,256]{1,0:T(8,128)S(1)}, s32[20,256]{1,0:T(8,128)}, u32[]{:S(2)}) copy-start(s32[20,256]{1,0:T(8,128)} %param.23) | copy-start | bytes 61444
  43.6 16.2 %copy-start.3 = (s32[2,128]{1,0:T(2,128)S(1)}, s32[2,128]{1,0:T(2,128)}, u32[]{:S(2)}) copy-start(s32[2,128]{1,0:T(2,128)} %param.24) | copy-start | bytes 3076
  43.6 17.5 %copy-start.1 = (f32[3,1024]{1,0:T(4,128)S(1)}, f32[3,1024]{1,0:T(4,128)}, u32[]{:S(2)}) copy-start(f32[3,1024]{1,0:T(4,128)} %param.27) | copy-start | bytes 36868
  43.6 17.5 %copy-start.2 = (f32[3,1024]{1,0:T(4,128)S(1)}, f32[3,1024]{1,0:T(4,128)}, u32[]{:S(2)}) copy-start(f32[3,1024]{1,0:T(4,128)} %param.26) | copy-start | bytes 36868
  51.9 17.2 %all-to-all-start.1 = ((f32[8,32,256]{2,0,1:T(8,128)}), f32[8,32,256]{2,0,1:T(8,128)S(1)}, u32[]{:S(2)}, u32[]{:S(2)}) async-start(f32[8,32,256]{2,0,1:T(8,128)} %copy.31), calls=%async_computation.1 | async-start | bytes 524288 | tf_op jit(solution)/shard_map/all_to_all | solution.py:515
  63.2 25.5 %copy-start.4 = (f32[4,8,1]{1,0,2:T(4,128)S(1)}, f32[4,8,1]{1,0,2:T(4,128)}, u32[]{:S(2)}) copy-start(f32[4,8,1]{1,0,2:T(4,128)} %constant.143) | copy-start | bytes 388
  69.2 19.1 %all-to-all-start = ((f32[12,32,256]{2,0,1:T(8,128)}), f32[12,32,256]{2,0,1:T(8,128)S(1)}, u32[]{:S(2)}, u32[]{:S(2)}) async-start(f32[12,32,256]{2,0,1:T(8,128)} %copy.28), calls=%async_computation | async-start | bytes 1048576 | tf_op jit(solution)/shard_map/all_to_all | solution.py:514
where the time goes:
time: 202 us; the launch traced here: 201 us
  Pallas kernels  130 us (64%)
  matrix products  23.7 us (12%)
  waiting for transfers between devices  13.8 us (7%)
  other arithmetic  12.6 us (6%)
  starting transfers between devices  10.6 us (5%)
  local copies, waits for them, and re-layouts  9.76 us (5%)
    pallas_call x1, Pallas kernels, solid_steps(): pl.pallas_call(functools.partial(solid_kernel, (gx_size, yz_size)), in_sp...  53.4 us
    pallas_call x1, Pallas kernels, stencil_traction(): pl.pallas_call(traction_kernel, grid=(face_count // tile,), in_specs=[col...  39.5 us
    pallas_call x1, Pallas kernels, wall_points(): pl.pallas_call(return_kernel, grid=(face_count // tile,), in_specs=[colum...  37.2 us
    dot_general x2, matrix products, spread_cols(): lax.dot_general(masked, upper_hot, (((1,), (1,)), ((), ())), precision=la...  22.5 us
    all_to_all x1, waiting for transfers between devices, shards(): lax.all_to_all(load_buffer, ('gx', 'yz'), split_axis=1, concat_axis=1, ti...  11.3 us
    all_to_all x1, starting transfers between devices, shards(): lax.all_to_all(node_buffer, ('gx', 'yz'), split_axis=1, concat_axis=1, ti...  7.09 us
  transfers between devices with their start and end apart: 2, of which 2 were waited for; matrix products, arithmetic and copies ran while one was open for 6% of the time, Pallas kernels for 0%

commit v1 on v0

--- a/solution.py
+++ b/solution.py
@@ -59,14 +59,19 @@
     lanes_width = lower_hot.shape[0]
     upper_count = upper_hot.shape[0]
     comps = values.shape[0]
-    masked = (values[:, None, :] * lower_hot[None]).reshape(comps * lanes_width, -1)
+    head = lax.reduce_precision(values, 8, 7)
+    tail = lax.reduce_precision(values - head, 8, 7)
+    parts = jnp.concatenate([head, tail], axis=0).astype(jnp.bfloat16)
+    masked = (parts[:, None, :] * lower_hot.astype(jnp.bfloat16)[None]).reshape(
+        2 * comps * lanes_width, -1
+    )
     summed = lax.dot_general(
         masked,
-        upper_hot,
+        upper_hot.astype(jnp.bfloat16),
         (((1,), (1,)), ((), ())),
-        precision=lax.Precision.HIGHEST,
         preferred_element_type=jnp.float32,
     )
+    summed = summed[: comps * lanes_width] + summed[comps * lanes_width :]
     return (
         summed.reshape(comps, lanes_width, upper_count)
         .transpose(0, 2, 1)
@@ -100,26 +105,26 @@
     tile = hot.shape[0]
     entry_count = entries.shape[0]
     chunks = table.shape[1] // LANES
-    rows_ref[...] = jnp.dot(hot, table, preferred_element_type=jnp.float32)
     padded = jnp.concatenate(
         [entries, jnp.zeros((LANES - entry_count, tile), jnp.int32)], axis=0
     ).T
     low_ref[...] = lax.rem(padded, LANES)
     high_ref[...] = lax.div(padded, LANES)
-
-    def group(step, carry):
-        rows = pl.ds(pl.multiple_of(step * SUBLANES, SUBLANES), SUBLANES)
-        low = low_ref[rows, :]
-        high = high_ref[rows, :]
-        taken = jnp.zeros((SUBLANES, LANES), jnp.float32)
-        for chunk in range(chunks):
-            part = rows_ref[rows, chunk * LANES : (chunk + 1) * LANES]
-            part = jnp.take_along_axis(part, low, axis=1, mode="promise_in_bounds")
-            taken = jnp.where(high == chunk, part, taken)
-        value_ref[rows, :] = taken
-        return carry
-
-    lax.fori_loop(0, tile // SUBLANES, group, 0, unroll=8)
+    sub = math.gcd(tile, LANES)
+    for first in range(0, tile, sub):
+        rows_ref[first : first + sub, :] = jnp.dot(
+            hot[first : first + sub], table, preferred_element_type=jnp.float32
+        )
+        for start in range(first, first + sub, SUBLANES):
+            rows = slice(start, start + SUBLANES)
+            low = low_ref[rows, :]
+            high = high_ref[rows, :]
+            taken = jnp.zeros((SUBLANES, LANES), jnp.float32)
+            for chunk in range(chunks):
+                part = rows_ref[rows, chunk * LANES : (chunk + 1) * LANES]
+                part = jnp.take_along_axis(part, low, axis=1, mode="promise_in_bounds")
+                taken = jnp.where(high == chunk, part, taken)
+            value_ref[rows, :] = taken
     return value_ref[...].T[:entry_count]
 
 
@@ -161,7 +166,7 @@
 
 
 def face_tile(face_count):
-    return math.gcd(face_count, 256)
+    return math.gcd(face_count, 512)
 
 
 def tile_scratch(tile, width):

time: 202 us -> 199 us (0.985)
  Pallas kernels: 130 us -> 107 us
  other arithmetic: 12.6 us -> 30.8 us
  local copies, waits for them, and re-layouts: 9.76 us -> 14.7 us
  matrix products: 23.7 us -> 19.4 us
    mul x0 -> x2, other arithmetic: none -> 17.3 us  [spread_cols(): parts[:, None, :] * lower_hot.astype(jnp.bfloat16)[None]]
    pallas_call x1, Pallas kernels: 37.2 us -> 24.6 us  [wall_points(): pl.pallas_call(return_kernel, grid=(face_count // tile,), in_specs=[colum...]
    pallas_call x1, Pallas kernels: 39.5 us -> 29 us  [stencil_traction(): pl.pallas_call(traction_kernel, grid=(face_count // tile,), in_specs=[col...]
    dot_general x2, matrix products: 22.5 us -> 18.2 us  [spread_cols(): lax.dot_general(masked, upper_hot.astype(jnp.bfloat16), (((1,), (1,)), ((...]
    all_to_all x1, waiting for transfers between devices: 2.48 us -> 0.35 us  [shards(): lax.all_to_all(node_buffer, ('gx', 'yz'), split_axis=1, concat_axis=1, ti...]
where the time goes in v1:
time: 199 us
  Pallas kernels  107 us (54%)
  other arithmetic  30.8 us (15%)
  matrix products  19.4 us (10%)
  local copies, waits for them, and re-layouts  14.7 us (7%)
  waiting for transfers between devices  13 us (7%)
  starting transfers between devices  12.6 us (6%)
    pallas_call x1, Pallas kernels, solid_steps(): pl.pallas_call(functools.partial(solid_kernel, (gx_size, yz_size)), in_sp...  53.4 us
    pallas_call x1, Pallas kernels, stencil_traction(): pl.pallas_call(traction_kernel, grid=(face_count // tile,), in_specs=[col...  29 us
    pallas_call x1, Pallas kernels, wall_points(): pl.pallas_call(return_kernel, grid=(face_count // tile,), in_specs=[colum...  24.6 us
    dot_general x2, matrix products, spread_cols(): lax.dot_general(masked, upper_hot.astype(jnp.bfloat16), (((1,), (1,)), ((...  18.2 us
    mul x2, other arithmetic, spread_cols(): parts[:, None, :] * lower_hot.astype(jnp.bfloat16)[None]  17.3 us
    all_to_all x1, waiting for transfers between devices, shards(): lax.all_to_all(load_buffer, ('gx', 'yz'), split_axis=1, concat_axis=1, ti...  12.6 us
    all_to_all x1, starting transfers between devices, shards(): lax.all_to_all(node_buffer, ('gx', 'yz'), split_axis=1, concat_axis=1, ti...  7.08 us
    all_to_all x1, starting transfers between devices, shards(): lax.all_to_all(load_buffer, ('gx', 'yz'), split_axis=1, concat_axis=1, ti...  5.49 us
  transfers between devices with their start and end apart: 2, of which 2 were waited for; matrix products, arithmetic and copies ran while one was open for 6% of the time, Pallas kernels for 0%

profile of v1, /device:TPU:1, one launch (start us, length us, event | category | flops | bytes accessed | tf_op | source)
XLA Modules:
  0.0 198.5 jit_solution(16804166983547601073)
XLA Ops:
  1.1 1.4 fusion.32
  3.2 0.9 convert_element_type.103
  4.1 29.0 %shard_map.158 = f32[12,4096]{1,0:T(8,128)} custom-call(s32[1,4096]{1,0:T(1,128)} %bitcast.62, s32[32,4096]{1,0:T(8,128)} %local_ref.1, f32[32,4096]{1,0:T(8,128)} %weight_ref.1, f32[12,4096]{1,0:T(8,128)} %normal_ref.1, bf16[256,4096]{1,0:T(8,128)(2,1)} %pressure_ref.1), custom_call_target="tpu_custom_call" | custom-call | flops 8589934592 | bytes 4194304 | tf_op jit(solution)/shard_map/pallas_call | solution.py:193
  33.2 1.0 reduce-precision_convert_fusion.1
  34.3 4.9 %broadcast_multiply_fusion.1 = bf16[40,32,4096]{2,1,0:T(8,128)(2,1)} fusion(bf16[32,4096]{1,0:T(8,128)(2,1)S(1)} %convert_convert_fusion.5, bf16[40,4096]{1,0:T(8,128)(2,1)S(1)} %pad_maximum_fusion.2), kind=kLoop, calls=%fused_computation.6 | loop fusion | flops 5242880 | bytes 11075584 | tf_op jit(solution)/shard_map/mul | solution.py:65
  39.2 5.6 %fusion.3 = f32[1280,256]{1,0:T(8,128)S(1)} fusion(bf16[1280,4096]{1,0:T(8,128)(2,1)} %bitcast.46, s32[4096]{0:T(1024)S(1)} %get-tuple-element.14), kind=kOutput, calls=%fused_computation.13 | convolution fusion | flops 2687500288 | bytes 11812864 | tf_op jit(solution)/shard_map/dot_general | solution.py:68
  45.0 0.9 copy.25
  45.9 1.0 slice.29
  46.9 1.5 reshape.302
  49.3 7.1 %all-to-all-start.1 = ((f32[8,32,256]{2,0,1:T(8,128)}), f32[8,32,256]{2,0,1:T(8,128)S(1)}, u32[]{:S(2)}, u32[]{:S(2)}) async-start(f32[8,32,256]{2,0,1:T(8,128)} %copy.28), calls=%async_computation.1 | async-start | bytes 524288 | tf_op jit(solution)/shard_map/all_to_all | solution.py:520
  59.6 1.3 slice.28
  60.9 1.9 reshape.299
  62.7 1.0 copy.26
  64.5 1.6 fusion.2.lower_ref
  66.5 5.5 %all-to-all-start = ((f32[12,32,256]{2,0,1:T(8,128)}), f32[12,32,256]{2,0,1:T(8,128)S(1)}, u32[]{:S(2)}, u32[]{:S(2)}) async-start(f32[12,32,256]{2,0,1:T(8,128)} %copy.26), calls=%async_computation | async-start | bytes 1048576 | tf_op jit(solution)/shard_map/all_to_all | solution.py:519
  72.5 2.6 %convert_convert_fusion.1 = bf16[32,65536]{1,0:T(8,128)(2,1)} fusion(s32[65536]{0:T(1024)S(1)} %get-tuple-element.11), kind=kLoop, calls=%fused_computation.4 | loop fusion | flops 6291456 | bytes 4456448 | tf_op jit(solution)/shard_map/convert_element_type | solution.py:65
  75.2 12.6 %all-to-all-done = f32[12,32,256]{2,0,1:T(8,128)S(1)} async-done(((f32[12,32,256]{2,0,1:T(8,128)}), f32[12,32,256]{2,0,1:T(8,128)S(1)}, u32[]{:S(2)}, u32[]{:S(2)}) %all-to-all-start) | async-done | bytes 393248 | tf_op jit(solution)/shard_map/all_to_all | solution.py:519
  89.9 1.5 pad_maximum_fusion
  91.4 12.4 %broadcast_multiply_fusion = bf16[6,32,65536]{2,1,0:T(8,128)(2,1)} fusion(bf16[32,65536]{1,0:T(8,128)(2,1)S(1)} %copy-done, bf16[6,65536]{1,0:T(8,128)(2,1)} %pad_maximum_fusion), kind=kLoop, calls=%fused_computation | loop fusion | flops 12582912 | bytes 30146560 | tf_op jit(solution)/shard_map/mul | solution.py:65
  103.9 12.6 %fusion = f32[192,32]{0,1:T(8,128)S(1)} fusion(bf16[192,65536]{1,0:T(8,128)(2,1)} %bitcast.45, s32[65536]{0:T(1024)S(1)} %get-tuple-element.10), kind=kOutput, calls=%fused_computation.7 | convolution fusion | flops 811597824 | bytes 25452544 | tf_op jit(solution)/shard_map/dot_general | solution.py:68
  117.3 53.4 %shard_map.159 = (f32[32,24,128]{2,1,0:T(8,128)}, f32[24,128]{1,0:T(8,128)}) custom-call(f32[60,60,256]{2,1,0:T(8,128)} %stiff_ref.1, s32[64,256]{1,0:T(8,128)} %get-tuple-element.13.low_ref, s32[64,256]{1,0:T(8,128)} %get-tuple-element.12.high_ref, f32[20,16,256]{2,1,0:T(8,128)} %fusion.15.upper_ref, bf16[20,128,256]{2,1,0:T(8,128)(2,1)} %fusion.2.lower_ref, ...), custom_call_target="tpu_custom_call" | custom-call | flops 7372800 | bytes 3686400 | tf_op jit(solution)/shard_map/pallas_call | solution.py:461
  170.8 1.8 copy.40
  172.6 1.3 reshape.307
  173.9 24.6 %shard_map.160 = f32[12,4096]{1,0:T(8,128)} custom-call(s32[1,4096]{1,0:T(1,128)} %bitcast.60, s32[8,4096]{1,0:T(8,128)} %nodes_ref.1, f32[12,24]{1,0:T(8,128)} %constant.138.clone.shape_ref, f32[32,3072]{1,0:T(8,128)} %bitcast.54), custom_call_target="tpu_custom_call" | custom-call | flops 1610612736 | bytes 393216 | tf_op jit(solution)/shard_map/pallas_call | solution.py:219
  (48 shorter events, 9.9 us)
Async XLA Ops:
  44.9 11.5 %copy-start.1 = (s32[20,256]{1,0:T(8,128)S(1)}, s32[20,256]{1,0:T(8,128)}, u32[]{:S(2)}) copy-start(s32[20,256]{1,0:T(8,128)} %param.23) | copy-start | bytes 61444
  44.9 12.2 %copy-start.4 = (s32[2,128]{1,0:T(2,128)S(1)}, s32[2,128]{1,0:T(2,128)}, u32[]{:S(2)}) copy-start(s32[2,128]{1,0:T(2,128)} %param.24) | copy-start | bytes 3076
  44.9 13.5 %copy-start.2 = (f32[3,1024]{1,0:T(4,128)S(1)}, f32[3,1024]{1,0:T(4,128)}, u32[]{:S(2)}) copy-start(f32[3,1024]{1,0:T(4,128)} %param.27) | copy-start | bytes 36868
  44.9 13.5 %copy-start.3 = (f32[3,1024]{1,0:T(4,128)S(1)}, f32[3,1024]{1,0:T(4,128)}, u32[]{:S(2)}) copy-start(f32[3,1024]{1,0:T(4,128)} %param.26) | copy-start | bytes 36868
  49.3 17.2 %all-to-all-start.1 = ((f32[8,32,256]{2,0,1:T(8,128)}), f32[8,32,256]{2,0,1:T(8,128)S(1)}, u32[]{:S(2)}, u32[]{:S(2)}) async-start(f32[8,32,256]{2,0,1:T(8,128)} %copy.28), calls=%async_computation.1 | async-start | bytes 524288 | tf_op jit(solution)/shard_map/all_to_all | solution.py:520
  66.5 21.2 %all-to-all-start = ((f32[12,32,256]{2,0,1:T(8,128)}), f32[12,32,256]{2,0,1:T(8,128)S(1)}, u32[]{:S(2)}, u32[]{:S(2)}) async-start(f32[12,32,256]{2,0,1:T(8,128)} %copy.26), calls=%async_computation | async-start | bytes 1048576 | tf_op jit(solution)/shard_map/all_to_all | solution.py:519
  72.0 16.2 %copy-start.5 = (f32[4,8,1]{1,0,2:T(4,128)S(1)}, f32[4,8,1]{1,0,2:T(4,128)}, u32[]{:S(2)}) copy-start(f32[4,8,1]{1,0,2:T(4,128)} %constant.143) | copy-start | bytes 388
  88.2 3.2 %copy-start = (bf16[32,65536]{1,0:T(8,128)(2,1)S(1)}, bf16[32,65536]{1,0:T(8,128)(2,1)}, u32[]{:S(2)}) copy-start(bf16[32,65536]{1,0:T(8,128)(2,1)} %convert_convert_fusion.1) | copy-start | bytes 12582916
